TPU v7x, 32 devices: a whole 2x2x4 slice. The times are simulated.
32 devices in a mesh: slab: 2 (over y), date: 8 (over z, x), tile: 1, sub: 2 (over core).
Axes of the slice: x: 2, y: 2, z: 4, core: 2. Of those that a mesh axis runs over, the one named last changes fastest.
Arguments:
- slc: bfloat16 [2, 100, 128, 512], P(None, None, 'date', ('slab', 'tile', 'sub')), parts along dimension 3, may hold values from -300 to 300, as said below
- usable: int32 [100, 128, 512], P(None, 'date', ('slab', 'tile', 'sub')), parts along dimension 2, may hold values 0 or 1
Outputs:
- coherence: bfloat16 [2, 4, 8, 16, 128, 128], P(None, ('slab', 'tile', 'sub'), 'date'), parts along dimension 1
- linked: float32 [2, 128, 512], P(None, 'date', ('slab', 'tile', 'sub')), parts along dimension 2
There are 2 independent parts, one for each index of `slab`. A program takes and returns all parts, laid end to end along the dimension named above; each array names one. Nothing has to cross between parts.
Inputs may be any that keep to these rules, and one draw needn't show every extreme that they name: `slc`: complex samples of a partly coherent stack.
All inputs are finite; a program needn't handle non-finite values. No bound on the sum of `usable` on one device may be relied on, other than what follows from the above.
Results may differ from a plain program's by a relative error of at most 0.0016.
Values may be sent and summed in bfloat16 or wider, within the bound.
No kernel may reach another device: no remote copies, remote signals or barrier semaphores. Data moves between devices by JAX's collectives and lax.ppermute only.
A program may use at most 64 MiB of HBM per device.

v0:
```python
import jax
import jax.numpy as jnp
from jax import lax
from jax.sharding import PartitionSpec as P

ITERS = 4


def inverse_roots(block):
    samples = block.astype(jnp.float32)
    intensity = jnp.mean(samples[0] * samples[0] + samples[1] * samples[1], axis=0) + 1e-05
    return lax.rsqrt(intensity)


def pair_terms(left_block, right_block, left_root, right_root, looks_count):
    real_sum = jnp.einsum(
        "law,lbw->wab", left_block[0], right_block[0], preferred_element_type=jnp.float32
    )
    real_sum = real_sum + jnp.einsum(
        "law,lbw->wab", left_block[1], right_block[1], preferred_element_type=jnp.float32
    )
    imag_sum = jnp.einsum(
        "law,lbw->wab", left_block[1], right_block[0], preferred_element_type=jnp.float32
    )
    imag_sum = imag_sum - jnp.einsum(
        "law,lbw->wab", left_block[0], right_block[1], preferred_element_type=jnp.float32
    )
    factor = left_root.T[:, :, None] * right_root.T[:, None, :] * (1.0 / looks_count)
    return jnp.stack([real_sum * factor, imag_sum * factor])


def local_pairs(samples, looks_count):
    window_root = inverse_roots(samples)
    return pair_terms(samples, samples, window_root, window_root, looks_count).astype(jnp.bfloat16)


def complex_apply(matrix, vec_real, vec_imag):
    rr = jnp.einsum("wab,bw->aw", matrix[0], vec_real, precision=lax.Precision.HIGHEST)
    ii = jnp.einsum("wab,bw->aw", matrix[1], vec_imag, precision=lax.Precision.HIGHEST)
    ri = jnp.einsum("wab,bw->aw", matrix[0], vec_imag, precision=lax.Precision.HIGHEST)
    ir = jnp.einsum("wab,bw->aw", matrix[1], vec_real, precision=lax.Precision.HIGHEST)
    return (rr - ii, ri + ir)


def local(slc, usable):
    masked = slc * usable.astype(jnp.bfloat16)[None]
    looks_count = slc.shape[1]
    own_dates = slc.shape[2]
    windows = slc.shape[3]
    blocks_count = lax.axis_size("date")
    all_dates = own_dates * blocks_count
    per_device = windows // blocks_count
    split_view = masked.reshape(2, looks_count, own_dates, blocks_count, per_device)
    result = local_pairs(
        lax.all_to_all(split_view, "date", split_axis=3, concat_axis=2, tiled=True)[:, :, :, 0, :],
        looks_count,
    )
    matrix = result.astype(jnp.float32)
    vec_real = jnp.ones((all_dates, per_device), jnp.float32)
    vec_imag = jnp.zeros((all_dates, per_device), jnp.float32)
    for step in range(ITERS):
        new_real, new_imag = complex_apply(matrix, vec_real, vec_imag)
        scale = lax.rsqrt(jnp.mean(new_real * new_real + new_imag * new_imag, axis=0) + 1e-05)
        vec_real = new_real * scale[None]
        vec_imag = new_imag * scale[None]
    linked = lax.all_to_all(
        jnp.stack([vec_real, vec_imag]), "date", split_axis=1, concat_axis=2, tiled=True
    )
    return (result.reshape(2, 1, 1, per_device, all_dates, all_dates), linked)


def solution(mesh):
    return jax.shard_map(
        local,
        mesh=mesh,
        in_specs=(
            P(None, None, "date", ("slab", "tile", "sub")),
            P(None, "date", ("slab", "tile", "sub")),
        ),
        out_specs=(
            P(None, ("slab", "tile", "sub"), "date", None, None, None),
            P(None, "date", ("slab", "tile", "sub")),
        ),
        check_vma=False,
    )
```

profile of v0, /device:TPU:0, one launch (start us, length us, event | category | flops | bytes accessed | tf_op | source)
XLA Modules:
  0.0 69.2 jit_solution(11306917477091956717)
XLA Ops:
  0.6 0.0 copy-start
  0.6 1.9 %copy.78 = bf16[2,100,16,128]{1,3,2,0:T(8,128)(2,1)S(1)} copy(bf16[2,100,16,128]{3,2,1,0:T(8,128)(2,1)} %param.2) | data formatting | bytes 1638400 | tf_op args[0]
  2.6 0.0 copy-done
  2.6 0.1 convert_element_type.16
  2.7 0.4 copy.77
  3.1 0.1 broadcast_multiply_fusion
  3.2 0.3 copy.79
  3.5 32.8 %all_to_all.33 = bf16[2,100,16,8,16]{1,4,2,0,3:T(8,128)(2,1)S(1)} all-to-all(bf16[2,100,16,8,16]{1,4,2,0,3:T(8,128)(2,1)S(1)} %copy.79), channel_id=1, replica_groups=mesh['slab'=2,'date'=8,'tile'=1,'sub'=2] {'date'}, dimensions={3} | all-to-all | bytes 1638400 | tf_op jit(solution)/shard_map/all_to_all | solution.py:55
  36.3 0.2 fusion.20
  36.6 0.5 copy.80
  37.1 0.5 copy.82
  37.6 0.2 bitcast_convert_fusion
  37.9 0.4 fusion.5
  38.3 0.1 copy.85
  38.4 0.1 reshape.89
  38.5 0.4 fusion.22
  38.8 0.5 fusion.3
  39.3 0.9 %fusion.10 = f32[16,1,128]{2,1,0:T(1,128)S(1)} fusion(bf16[16,128,128]{2,1,0:T(8,128)(2,1)S(1)} %fusion.3), kind=kOutput, calls=%fused_computation.26 | convolution fusion | flops 3145728 | bytes 532480 | tf_op jit(solution)/shard_map/wab,bw->aw/dot_general | solution.py:39
  40.3 0.9 %fusion.12 = f32[16,1,128]{2,1,0:T(1,128)S(1)} fusion(bf16[16,128,128]{2,1,0:T(8,128)(2,1)S(1)} %fusion.3), kind=kOutput, calls=%fused_computation.28 | convolution fusion | flops 3145728 | bytes 532480 | tf_op jit(solution)/shard_map/wab,bw->aw/dot_general | solution.py:41
  41.2 0.4 fusion.21
  41.6 0.5 fusion.2
  42.1 0.9 %fusion.14 = f32[16,1,128]{2,1,0:T(1,128)S(1)} fusion(bf16[16,128,128]{2,1,0:T(8,128)(2,1)S(1)} %fusion.2), kind=kOutput, calls=%fused_computation.30 | convolution fusion | flops 3145728 | bytes 532480 | tf_op jit(solution)/shard_map/wab,bw->aw/dot_general | solution.py:38
  43.0 0.9 %fusion.8 = f32[16,1,128]{2,1,0:T(1,128)S(1)} fusion(bf16[16,128,128]{2,1,0:T(8,128)(2,1)S(1)} %fusion.2), kind=kOutput, calls=%fused_computation.24 | convolution fusion | flops 3145728 | bytes 532480 | tf_op jit(solution)/shard_map/wab,bw->aw/dot_general | solution.py:40
  43.9 0.1 add_reduce_fusion.3
  44.1 0.1 broadcast_multiply_fusion.5
  44.1 0.9 %fusion.25 = f32[16,1,128]{2,1,0:T(1,128)S(1)} fusion(f32[128,16,1]{0,2,1:T(1,128)S(1)} %bitcast.144, bf16[16,128,128]{2,1,0:T(8,128)(2,1)S(1)} %fusion.2), kind=kOutput, calls=%fused_computation.52 | convolution fusion | flops 3145728 | bytes 540672 | tf_op jit(solution)/shard_map/wab,bw->aw/dot_general | solution.py:40
  45.1 0.9 %fusion.24 = f32[16,1,128]{2,1,0:T(1,128)S(1)} fusion(f32[128,16,1]{0,2,1:T(1,128)S(1)} %bitcast.145, bf16[16,128,128]{2,1,0:T(8,128)(2,1)S(1)} %fusion.3), kind=kOutput, calls=%fused_computation.51 | convolution fusion | flops 3145728 | bytes 540672 | tf_op jit(solution)/shard_map/wab,bw->aw/dot_general | solution.py:39
  46.0 0.9 %fusion.26 = f32[16,1,128]{2,1,0:T(1,128)S(1)} fusion(f32[128,16,1]{0,2,1:T(1,128)S(1)} %bitcast.138, bf16[16,128,128]{2,1,0:T(8,128)(2,1)S(1)} %fusion.3), kind=kOutput, calls=%fused_computation.53 | convolution fusion | flops 3145728 | bytes 540672 | tf_op jit(solution)/shard_map/wab,bw->aw/dot_general | solution.py:41
  46.9 0.9 %fusion.23 = f32[16,1,128]{2,1,0:T(1,128)S(1)} fusion(f32[128,16,1]{0,2,1:T(1,128)S(1)} %bitcast.139, bf16[16,128,128]{2,1,0:T(8,128)(2,1)S(1)} %fusion.2), kind=kOutput, calls=%fused_computation.50 | convolution fusion | flops 3145728 | bytes 540672 | tf_op jit(solution)/shard_map/wab,bw->aw/dot_general | solution.py:38
  47.8 0.1 add_reduce_fusion.2
  48.0 0.1 broadcast_multiply_fusion.3
  48.0 0.9 %fusion.29 = f32[16,1,128]{2,1,0:T(1,128)S(1)} fusion(f32[128,16,1]{0,2,1:T(1,128)S(1)} %bitcast.146, bf16[16,128,128]{2,1,0:T(8,128)(2,1)S(1)} %fusion.2), kind=kOutput, calls=%fused_computation.56 | convolution fusion | flops 3145728 | bytes 540672 | tf_op jit(solution)/shard_map/wab,bw->aw/dot_general | solution.py:40
  49.0 0.9 %fusion.28 = f32[16,1,128]{2,1,0:T(1,128)S(1)} fusion(f32[128,16,1]{0,2,1:T(1,128)S(1)} %bitcast.147, bf16[16,128,128]{2,1,0:T(8,128)(2,1)S(1)} %fusion.3), kind=kOutput, calls=%fused_computation.55 | convolution fusion | flops 3145728 | bytes 540672 | tf_op jit(solution)/shard_map/wab,bw->aw/dot_general | solution.py:39
  49.9 0.9 %fusion.30 = f32[16,1,128]{2,1,0:T(1,128)S(1)} fusion(f32[128,16,1]{0,2,1:T(1,128)S(1)} %bitcast.140, bf16[16,128,128]{2,1,0:T(8,128)(2,1)S(1)} %fusion.3), kind=kOutput, calls=%fused_computation.57 | convolution fusion | flops 3145728 | bytes 540672 | tf_op jit(solution)/shard_map/wab,bw->aw/dot_general | solution.py:41
  50.8 0.9 %fusion.27 = f32[16,1,128]{2,1,0:T(1,128)S(1)} fusion(f32[128,16,1]{0,2,1:T(1,128)S(1)} %bitcast.141, bf16[16,128,128]{2,1,0:T(8,128)(2,1)S(1)} %fusion.2), kind=kOutput, calls=%fused_computation.54 | convolution fusion | flops 3145728 | bytes 540672 | tf_op jit(solution)/shard_map/wab,bw->aw/dot_general | solution.py:38
  51.7 0.1 add_reduce_fusion.1
  51.9 0.1 broadcast_multiply_fusion.1
  52.0 0.9 %fusion.33 = f32[16,1,128]{2,1,0:T(1,128)S(1)} fusion(f32[128,16,1]{0,2,1:T(1,128)S(1)} %bitcast.148, bf16[16,128,128]{2,1,0:T(8,128)(2,1)S(1)} %fusion.2), kind=kOutput, calls=%fused_computation.60 | convolution fusion | flops 3145728 | bytes 540672 | tf_op jit(solution)/shard_map/wab,bw->aw/dot_general | solution.py:40
  52.9 0.9 %fusion.32 = f32[16,1,128]{2,1,0:T(1,128)S(1)} fusion(f32[128,16,1]{0,2,1:T(1,128)S(1)} %bitcast.149, bf16[16,128,128]{2,1,0:T(8,128)(2,1)S(1)} %fusion.3), kind=kOutput, calls=%fused_computation.59 | convolution fusion | flops 3145728 | bytes 540672 | tf_op jit(solution)/shard_map/wab,bw->aw/dot_general | solution.py:39
  53.8 0.9 %fusion.34 = f32[16,1,128]{2,1,0:T(1,128)S(1)} fusion(f32[128,16,1]{0,2,1:T(1,128)S(1)} %bitcast.142, bf16[16,128,128]{2,1,0:T(8,128)(2,1)S(1)} %fusion.3), kind=kOutput, calls=%fused_computation.61 | convolution fusion | flops 3145728 | bytes 540672 | tf_op jit(solution)/shard_map/wab,bw->aw/dot_general | solution.py:41
  54.7 0.9 %fusion.31 = f32[16,1,128]{2,1,0:T(1,128)S(1)} fusion(f32[128,16,1]{0,2,1:T(1,128)S(1)} %bitcast.143, bf16[16,128,128]{2,1,0:T(8,128)(2,1)S(1)} %fusion.2), kind=kOutput, calls=%fused_computation.58 | convolution fusion | flops 3145728 | bytes 540672 | tf_op jit(solution)/shard_map/wab,bw->aw/dot_general | solution.py:38
  55.7 0.1 add_reduce_fusion
  55.8 0.1 multiply_bitcast_fusion.1
  55.9 0.1 copy.90
  56.0 0.8 %reshape.118 = f32[8,1,512]{2,1,0:T(1,128)} reshape(f32[128,2,16]{2,1,0:T(2,128)S(1)} %bitcast.133) | data formatting | bytes 32768
  56.8 3.6 %all-to-all-start.1 = ((f32[8,1,512]{2,1,0:T(1,128)}), f32[8,1,512]{2,1,0:T(1,128)S(1)}, u32[]{:S(2)}, u32[]{:S(2)}) async-start(f32[8,1,512]{2,1,0:T(1,128)} %reshape.118), calls=%async_computation.1 | async-start | bytes 32768 | tf_op jit(solution)/shard_map/all_to_all | solution.py:66
  60.4 1.1 %pad_maximum_fusion = bf16[2,1,1,16,128,128]{5,4,3,2,1,0:T(8,128)(2,1)} fusion(bf16[1,1,1,16,128,128]{5,4,3,2,1,0:T(8,128)(2,1)S(1)} %bitcast.127, bf16[1,1,1,16,128,128]{5,4,3,2,1,0:T(8,128)(2,1)S(1)} %bitcast.128), kind=kLoop, calls=%fused_computation.10 | loop fusion | flops 524288 | bytes 2097152 | tf_op jit(solution)/shard_map/stack | solution.py:29
  61.5 5.5 %all-to-all-done.1 = f32[8,1,512]{2,1,0:T(1,128)S(1)} async-done(((f32[8,1,512]{2,1,0:T(1,128)}), f32[8,1,512]{2,1,0:T(1,128)S(1)}, u32[]{:S(2)}, u32[]{:S(2)}) %all-to-all-start.1) | async-done | bytes 16416 | tf_op jit(solution)/shard_map/all_to_all | solution.py:66
  67.0 0.5 broadcast.84
  67.5 0.7 reduce.7
  68.2 0.2 reshape.119
  68.4 0.1 copy.131
  68.5 0.7 %all_to_all.30 = f32[2,16,128]{2,1,0:T(8,128)} reshape(f32[2,16,8,16]{3,2,1,0:T(8,128)S(1)} %bitcast.135) | data formatting | bytes 32768 | tf_op jit(solution)/shard_map/all_to_all | solution.py:66
  (6 shorter events, 0.1 us)
Async XLA Ops:
  0.6 2.0 %copy-start = (s32[100,16,128]{2,1,0:T(8,128)S(1)}, s32[100,16,128]{2,1,0:T(8,128)}, u32[]{:S(2)}) copy-start(s32[100,16,128]{2,1,0:T(8,128)} %param.3) | copy-start | bytes 2457604
  56.8 10.2 %all-to-all-start.1 = ((f32[8,1,512]{2,1,0:T(1,128)}), f32[8,1,512]{2,1,0:T(1,128)S(1)}, u32[]{:S(2)}, u32[]{:S(2)}) async-start(f32[8,1,512]{2,1,0:T(1,128)} %reshape.118), calls=%async_computation.1 | async-start | bytes 32768 | tf_op jit(solution)/shard_map/all_to_all | solution.py:66
where the time goes:
time: 69.4 us; the launch traced here: 69.2 us
  blocking collectives  32.8 us (47%)
  matrix products  16.5 us (24%)
  local copies, waits for them, and re-layouts  6.56 us (9%)
  waiting for transfers between devices  5.51 us (8%)
  starting transfers between devices  3.59 us (5%)
  other arithmetic  3.35 us (5%)
  between operations  0.82 us (1%)
    all_to_all x1, blocking collectives, local(): lax.all_to_all(split_view, 'date', split_axis=3, concat_axis=2, tiled=True)  32.8 us
    all_to_all x1, waiting for transfers between devices, local(): lax.all_to_all(jnp.stack([vec_real, vec_imag]), 'date', split_axis=1, con...  5.51 us
    dot_general x4, matrix products, complex_apply(): jnp.einsum('wab,bw->aw', matrix[1], vec_real, precision=lax.Precision.HIG...  3.7 us
    dot_general x4, matrix products, complex_apply(): jnp.einsum('wab,bw->aw', matrix[0], vec_imag, precision=lax.Precision.HIG...  3.68 us
    dot_general x4, matrix products, complex_apply(): jnp.einsum('wab,bw->aw', matrix[0], vec_real, precision=lax.Precision.HIG...  3.68 us
    dot_general x4, matrix products, complex_apply(): jnp.einsum('wab,bw->aw', matrix[1], vec_imag, precision=lax.Precision.HIG...  3.68 us
    all_to_all x1, starting transfers between devices, local(): lax.all_to_all(jnp.stack([vec_real, vec_imag]), 'date', split_axis=1, con...  3.59 us
    unnamed x5, local copies, waits for them, and re-layouts  2.95 us
  transfers between devices with their start and end apart: 1, of which 1 were waited for; matrix products, arithmetic and copies ran while one was open for 2% of the time, Pallas kernels for 0%

commit v1 on v0

--- a/solution.py
+++ b/solution.py
@@ -63,9 +63,16 @@
         scale = lax.rsqrt(jnp.mean(new_real * new_real + new_imag * new_imag, axis=0) + 1e-05)
         vec_real = new_real * scale[None]
         vec_imag = new_imag * scale[None]
-    linked = lax.all_to_all(
-        jnp.stack([vec_real, vec_imag]), "date", split_axis=1, concat_axis=2, tiled=True
-    )
+    x = jnp.stack([vec_real, vec_imag])
+    ways, here = (lax.axis_size("date"), lax.axis_index("date"))
+    width = x.shape[1] // ways
+    turned = jnp.roll(x, -here * width, axis=1)
+    got = [lax.slice_in_dim(turned, 0, width, axis=1)]
+    for far in range(1, ways):
+        sent = lax.slice_in_dim(turned, far * width, (far + 1) * width, axis=1)
+        got.append(lax.ppermute(sent, "date", [(d, (d + far) % ways) for d in range(ways)]))
+    line = jnp.concatenate(got[::-1], axis=2)
+    linked = jnp.roll(line, (here + 1) * got[0].shape[2], axis=2)
     return (result.reshape(2, 1, 1, per_device, all_dates, all_dates), linked)
 
 

time: 69.4 us -> 72.1 us (1.039)
  blocking collectives: 32.8 us -> 0 us
  waiting for transfers between devices: 5.51 us -> 29.2 us
  starting transfers between devices: 3.59 us -> 16.1 us
    all_to_all x1 -> x0, blocking collectives: 32.8 us -> none  [local(): lax.all_to_all(split_view, 'date', split_axis=3, concat_axis=2, tiled=True)]
    all_to_all x1, waiting for transfers between devices: 5.51 us -> 25.8 us  [local(): lax.all_to_all(split_view, 'date', split_axis=3, concat_axis=2, tiled=True)]
    ppermute x0 -> x7, starting transfers between devices: none -> 8.78 us  [local(): lax.ppermute(sent, 'date', [(d, (d + far) % ways) for d in range(ways)])]
    all_to_all x1, starting transfers between devices: 3.59 us -> 7.28 us  [local(): lax.all_to_all(split_view, 'date', split_axis=3, concat_axis=2, tiled=True)]
    ppermute x0 -> x7, waiting for transfers between devices: none -> 3.48 us  [local(): lax.ppermute(sent, 'date', [(d, (d + far) % ways) for d in range(ways)])]
    all_to_all x3 -> x0, local copies, waits for them, and re-layouts: 1.3 us -> none  [local(): lax.all_to_all(jnp.stack([vec_real, vec_imag]), 'date', split_axis=1, con...]
    unnamed x5 -> x3, local copies, waits for them, and re-layouts: 2.95 us -> 1.94 us
    reshape x1, local copies, waits for them, and re-layouts: 0.27 us -> 1.24 us  [local(): masked.reshape(2, looks_count, own_dates, blocks_count, per_device)]
  transfers between devices with their start and end apart: 1 -> 8, of which waited for: 1 -> 4; matrix products, arithmetic and copies ran while one was open for 2% -> 2% of each run, Pallas kernels for 0% -> 0%
where the time goes in v1:
time: 72.1 us; the launch traced here: 72 us
  waiting for transfers between devices  29.2 us (40%)
  matrix products  16.5 us (23%)
  starting transfers between devices  16.1 us (22%)
  local copies, waits for them, and re-layouts  6.56 us (9%)
  other arithmetic  2.74 us (4%)
  between operations  0.81 us (1%)
    all_to_all x1, waiting for transfers between devices, local(): lax.all_to_all(split_view, 'date', split_axis=3, concat_axis=2, tiled=True)  25.8 us
    ppermute x7, starting transfers between devices, local(): lax.ppermute(sent, 'date', [(d, (d + far) % ways) for d in range(ways)])  8.78 us
    all_to_all x1, starting transfers between devices, local(): lax.all_to_all(split_view, 'date', split_axis=3, concat_axis=2, tiled=True)  7.28 us
    dot_general x4, matrix products, complex_apply(): jnp.einsum('wab,bw->aw', matrix[0], vec_imag, precision=lax.Precision.HIG...  3.7 us
    dot_general x4, matrix products, complex_apply(): jnp.einsum('wab,bw->aw', matrix[1], vec_real, precision=lax.Precision.HIG...  3.7 us
    dot_general x4, matrix products, complex_apply(): jnp.einsum('wab,bw->aw', matrix[1], vec_imag, precision=lax.Precision.HIG...  3.68 us
    dot_general x4, matrix products, complex_apply(): jnp.einsum('wab,bw->aw', matrix[0], vec_real, precision=lax.Precision.HIG...  3.67 us
    ppermute x7, waiting for transfers between devices, local(): lax.ppermute(sent, 'date', [(d, (d + far) % ways) for d in range(ways)])  3.48 us
  transfers between devices with their start and end apart: 8, of which 4 were waited for; matrix products, arithmetic and copies ran while one was open for 2% of the time, Pallas kernels for 0%

profile of v1, /device:TPU:0, one launch (start us, length us, event | category | flops | bytes accessed | tf_op | source)
XLA Modules:
  0.0 72.0 jit_solution(125433265288515688)
XLA Ops:
  0.6 1.9 %copy.74 = bf16[2,100,16,128]{1,3,2,0:T(8,128)(2,1)S(1)} copy(bf16[2,100,16,128]{3,2,1,0:T(8,128)(2,1)} %param.2) | data formatting | bytes 1638400 | tf_op args[0]
  2.6 0.1 convert_element_type.16
  2.7 0.4 copy.73
  3.1 0.1 broadcast_multiply_fusion
  3.2 1.2 %copy.75 = bf16[2,100,16,8,16]{1,4,2,0,3:T(8,128)(2,1)} copy(bf16[2,100,16,8,16]{1,4,3,2,0:T(8,128)(2,1)S(1)} %bitcast.121) | data formatting | bytes 1638400 | tf_op jit(solution)/shard_map/reshape | solution.py:53
  4.5 7.3 %all-to-all-start = ((bf16[2,100,16,8,16]{1,4,2,0,3:T(8,128)(2,1)}), bf16[2,100,16,8,16]{1,4,2,0,3:T(8,128)(2,1)S(1)}, u32[]{:S(2)}, u32[]{:S(2)}) async-start(bf16[2,100,16,8,16]{1,4,2,0,3:T(8,128)(2,1)} %copy.75), calls=%async_computation | async-start | bytes 2097152 | tf_op jit(solution)/shard_map/all_to_all | solution.py:55
  11.7 25.8 %all-to-all-done = bf16[2,100,16,8,16]{1,4,2,0,3:T(8,128)(2,1)S(1)} async-done(((bf16[2,100,16,8,16]{1,4,2,0,3:T(8,128)(2,1)}), bf16[2,100,16,8,16]{1,4,2,0,3:T(8,128)(2,1)S(1)}, u32[]{:S(2)}, u32[]{:S(2)}) %all-to-all-start) | async-done | bytes 819232 | tf_op jit(solution)/shard_map/all_to_all | solution.py:55
  37.5 0.2 fusion.23
  37.8 0.5 copy.76
  38.3 0.5 copy.78
  38.8 0.2 bitcast_convert_fusion
  39.0 0.4 fusion.5
  39.4 0.1 copy.81
  39.6 0.1 reshape.89
  39.6 0.4 fusion.26
  40.0 0.5 fusion.3
  40.5 0.9 %fusion.13 = f32[16,1,128]{2,1,0:T(1,128)S(1)} fusion(bf16[16,128,128]{2,1,0:T(8,128)(2,1)S(1)} %fusion.3), kind=kOutput, calls=%fused_computation.31 | convolution fusion | flops 3145728 | bytes 532480 | tf_op jit(solution)/shard_map/wab,bw->aw/dot_general | solution.py:39
  41.4 0.9 %fusion.15 = f32[16,1,128]{2,1,0:T(1,128)S(1)} fusion(bf16[16,128,128]{2,1,0:T(8,128)(2,1)S(1)} %fusion.3), kind=kOutput, calls=%fused_computation.33 | convolution fusion | flops 3145728 | bytes 532480 | tf_op jit(solution)/shard_map/wab,bw->aw/dot_general | solution.py:41
  42.4 0.4 fusion.25
  42.7 0.5 fusion.2
  43.3 0.9 %fusion.17 = f32[16,1,128]{2,1,0:T(1,128)S(1)} fusion(bf16[16,128,128]{2,1,0:T(8,128)(2,1)S(1)} %fusion.2), kind=kOutput, calls=%fused_computation.35 | convolution fusion | flops 3145728 | bytes 532480 | tf_op jit(solution)/shard_map/wab,bw->aw/dot_general | solution.py:38
  44.2 0.9 %fusion.11 = f32[16,1,128]{2,1,0:T(1,128)S(1)} fusion(bf16[16,128,128]{2,1,0:T(8,128)(2,1)S(1)} %fusion.2), kind=kOutput, calls=%fused_computation.29 | convolution fusion | flops 3145728 | bytes 532480 | tf_op jit(solution)/shard_map/wab,bw->aw/dot_general | solution.py:40
  45.1 0.1 add_reduce_fusion.3
  45.2 0.1 broadcast_multiply_fusion.6
  45.3 0.9 %fusion.27 = f32[16,1,128]{2,1,0:T(1,128)S(1)} fusion(f32[128,16,1]{0,2,1:T(1,128)S(1)} %bitcast.132, bf16[16,128,128]{2,1,0:T(8,128)(2,1)S(1)} %fusion.2), kind=kOutput, calls=%fused_computation.57 | convolution fusion | flops 3145728 | bytes 540672 | tf_op jit(solution)/shard_map/wab,bw->aw/dot_general | solution.py:38
  46.2 0.9 %fusion.30 = f32[16,1,128]{2,1,0:T(1,128)S(1)} fusion(f32[128,16,1]{0,2,1:T(1,128)S(1)} %bitcast.133, bf16[16,128,128]{2,1,0:T(8,128)(2,1)S(1)} %fusion.3), kind=kOutput, calls=%fused_computation.60 | convolution fusion | flops 3145728 | bytes 540672 | tf_op jit(solution)/shard_map/wab,bw->aw/dot_general | solution.py:41
  47.2 0.9 %fusion.28 = f32[16,1,128]{2,1,0:T(1,128)S(1)} fusion(f32[128,16,1]{0,2,1:T(1,128)S(1)} %bitcast.126, bf16[16,128,128]{2,1,0:T(8,128)(2,1)S(1)} %fusion.3), kind=kOutput, calls=%fused_computation.58 | convolution fusion | flops 3145728 | bytes 540672 | tf_op jit(solution)/shard_map/wab,bw->aw/dot_general | solution.py:39
  48.1 0.9 %fusion.29 = f32[16,1,128]{2,1,0:T(1,128)S(1)} fusion(f32[128,16,1]{0,2,1:T(1,128)S(1)} %bitcast.127, bf16[16,128,128]{2,1,0:T(8,128)(2,1)S(1)} %fusion.2), kind=kOutput, calls=%fused_computation.59 | convolution fusion | flops 3145728 | bytes 540672 | tf_op jit(solution)/shard_map/wab,bw->aw/dot_general | solution.py:40
  49.0 0.1 add_reduce_fusion.2
  49.1 0.1 broadcast_multiply_fusion.4
  49.2 0.9 %fusion.31 = f32[16,1,128]{2,1,0:T(1,128)S(1)} fusion(f32[128,16,1]{0,2,1:T(1,128)S(1)} %bitcast.134, bf16[16,128,128]{2,1,0:T(8,128)(2,1)S(1)} %fusion.2), kind=kOutput, calls=%fused_computation.61 | convolution fusion | flops 3145728 | bytes 540672 | tf_op jit(solution)/shard_map/wab,bw->aw/dot_general | solution.py:38
  50.1 0.9 %fusion.34 = f32[16,1,128]{2,1,0:T(1,128)S(1)} fusion(f32[128,16,1]{0,2,1:T(1,128)S(1)} %bitcast.135, bf16[16,128,128]{2,1,0:T(8,128)(2,1)S(1)} %fusion.3), kind=kOutput, calls=%fused_computation.64 | convolution fusion | flops 3145728 | bytes 540672 | tf_op jit(solution)/shard_map/wab,bw->aw/dot_general | solution.py:41
  51.1 0.9 %fusion.32 = f32[16,1,128]{2,1,0:T(1,128)S(1)} fusion(f32[128,16,1]{0,2,1:T(1,128)S(1)} %bitcast.128, bf16[16,128,128]{2,1,0:T(8,128)(2,1)S(1)} %fusion.3), kind=kOutput, calls=%fused_computation.62 | convolution fusion | flops 3145728 | bytes 540672 | tf_op jit(solution)/shard_map/wab,bw->aw/dot_general | solution.py:39
  52.0 0.9 %fusion.33 = f32[16,1,128]{2,1,0:T(1,128)S(1)} fusion(f32[128,16,1]{0,2,1:T(1,128)S(1)} %bitcast.129, bf16[16,128,128]{2,1,0:T(8,128)(2,1)S(1)} %fusion.2), kind=kOutput, calls=%fused_computation.63 | convolution fusion | flops 3145728 | bytes 540672 | tf_op jit(solution)/shard_map/wab,bw->aw/dot_general | solution.py:40
  52.9 0.1 add_reduce_fusion.1
  53.1 0.1 broadcast_multiply_fusion.2
  53.1 0.9 %fusion.35 = f32[16,1,128]{2,1,0:T(1,128)S(1)} fusion(f32[128,16,1]{0,2,1:T(1,128)S(1)} %bitcast.136, bf16[16,128,128]{2,1,0:T(8,128)(2,1)S(1)} %fusion.2), kind=kOutput, calls=%fused_computation.65 | convolution fusion | flops 3145728 | bytes 540672 | tf_op jit(solution)/shard_map/wab,bw->aw/dot_general | solution.py:38
  54.1 0.9 %fusion.38 = f32[16,1,128]{2,1,0:T(1,128)S(1)} fusion(f32[128,16,1]{0,2,1:T(1,128)S(1)} %bitcast.137, bf16[16,128,128]{2,1,0:T(8,128)(2,1)S(1)} %fusion.3), kind=kOutput, calls=%fused_computation.68 | convolution fusion | flops 3145728 | bytes 540672 | tf_op jit(solution)/shard_map/wab,bw->aw/dot_general | solution.py:41
  55.0 0.9 %fusion.36 = f32[16,1,128]{2,1,0:T(1,128)S(1)} fusion(f32[128,16,1]{0,2,1:T(1,128)S(1)} %bitcast.130, bf16[16,128,128]{2,1,0:T(8,128)(2,1)S(1)} %fusion.3), kind=kOutput, calls=%fused_computation.66 | convolution fusion | flops 3145728 | bytes 540672 | tf_op jit(solution)/shard_map/wab,bw->aw/dot_general | solution.py:39
  55.9 0.9 %fusion.37 = f32[16,1,128]{2,1,0:T(1,128)S(1)} fusion(f32[128,16,1]{0,2,1:T(1,128)S(1)} %bitcast.131, bf16[16,128,128]{2,1,0:T(8,128)(2,1)S(1)} %fusion.2), kind=kOutput, calls=%fused_computation.67 | convolution fusion | flops 3145728 | bytes 540672 | tf_op jit(solution)/shard_map/wab,bw->aw/dot_general | solution.py:40
  56.8 0.1 add_reduce_fusion
  57.0 0.1 multiply_bitcast_fusion
  57.0 0.1 fusion.9
  57.1 0.1 fusion.24
  57.2 2.4 %collective-permute-start = (f32[2,16,16]{1,2,0:T(8,128)S(1)}, f32[2,16,16]{1,2,0:T(8,128)S(1)}, u32[]{:S(2)}, u32[]{:S(2)}) collective-permute-start(f32[2,16,16]{1,2,0:T(8,128)S(1)} %get-tuple-element.27), channel_id=1, source_target_pairs={{0,14},{2,0},{4,2},{6,4},{8,6},{10,8},{12,10},{14,12},{1,15},{3,1}... | collective-permute-start | bytes 6152 | tf_op jit(solution)/shard_map/ppermute | solution.py:73
  59.6 0.0 collective-permute-start.1
  59.6 0.2 collective-permute-start.2
  59.8 3.0 %collective-permute-start.3 = (f32[2,16,16]{1,2,0:T(8,128)S(1)}, f32[2,16,16]{1,2,0:T(8,128)S(1)}, u32[]{:S(2)}, u32[]{:S(2)}) collective-permute-start(f32[2,16,16]{1,2,0:T(8,128)S(1)} %get-tuple-element.24), channel_id=1, source_target_pairs={{0,8},{2,10},{4,12},{6,14},{8,0},{10,2},{12,4},{14,6},{1,9},{3,11}... | collective-permute-start | bytes 6152 | tf_op jit(solution)/shard_map/ppermute | solution.py:73
  62.9 1.7 %collective-permute-start.4 = (f32[2,16,16]{1,2,0:T(8,128)S(1)}, f32[2,16,16]{1,2,0:T(8,128)S(1)}, u32[]{:S(2)}, u32[]{:S(2)}) collective-permute-start(f32[2,16,16]{1,2,0:T(8,128)S(1)} %get-tuple-element.23), channel_id=1, source_target_pairs={{0,6},{2,8},{4,10},{6,12},{8,14},{10,0},{12,2},{14,4},{1,7},{3,9},... | collective-permute-start | bytes 6152 | tf_op jit(solution)/shard_map/ppermute | solution.py:73
  64.6 1.5 %collective-permute-start.6 = (f32[2,16,16]{1,2,0:T(8,128)S(1)}, f32[2,16,16]{1,2,0:T(8,128)S(1)}, u32[]{:S(2)}, u32[]{:S(2)}) collective-permute-start(f32[2,16,16]{1,2,0:T(8,128)S(1)} %get-tuple-element.21), channel_id=1, source_target_pairs={{0,2},{2,4},{4,6},{6,8},{8,10},{10,12},{12,14},{14,0},{1,3},{3,5},... | collective-permute-start | bytes 6152 | tf_op jit(solution)/shard_map/ppermute | solution.py:73
  66.0 1.1 %pad_maximum_fusion = bf16[2,1,1,16,128,128]{5,4,3,2,1,0:T(8,128)(2,1)} fusion(bf16[1,1,1,16,128,128]{5,4,3,2,1,0:T(8,128)(2,1)S(1)} %bitcast.118, bf16[1,1,1,16,128,128]{5,4,3,2,1,0:T(8,128)(2,1)S(1)} %bitcast.119), kind=kLoop, calls=%fused_computation.10 | loop fusion | flops 524288 | bytes 2097152 | tf_op jit(solution)/shard_map/stack | solution.py:29
  67.1 0.1 copy.93
  67.2 0.1 copy.86
  67.2 0.1 copy.87
  67.3 0.1 copy.88
  67.4 0.1 copy.89
  67.5 0.9 %collective-permute-done.4 = f32[2,16,16]{1,2,0:T(8,128)S(1)} collective-permute-done((f32[2,16,16]{1,2,0:T(8,128)S(1)}, f32[2,16,16]{1,2,0:T(8,128)S(1)}, u32[]{:S(2)}, u32[]{:S(2)}) %collective-permute-start.4) | collective-permute-done | bytes 2080 | tf_op jit(solution)/shard_map/ppermute | solution.py:73
  68.4 0.1 copy.90
  68.5 1.6 %collective-permute-done.5 = f32[2,16,16]{1,2,0:T(8,128)S(1)} collective-permute-done((f32[2,16,16]{1,2,0:T(8,128)S(1)}, f32[2,16,16]{1,2,0:T(8,128)S(1)}, u32[]{:S(2)}, u32[]{:S(2)}) %collective-permute-start.5) | collective-permute-done | bytes 2080 | tf_op jit(solution)/shard_map/ppermute | solution.py:73
  70.1 0.1 copy.91
  70.2 0.9 %collective-permute-done.6 = f32[2,16,16]{1,2,0:T(8,128)S(1)} collective-permute-done((f32[2,16,16]{1,2,0:T(8,128)S(1)}, f32[2,16,16]{1,2,0:T(8,128)S(1)}, u32[]{:S(2)}, u32[]{:S(2)}) %collective-permute-start.6) | collective-permute-done | bytes 2080 | tf_op jit(solution)/shard_map/ppermute | solution.py:73
  71.1 0.1 copy.92
  71.1 0.1 concatenate.19
  71.3 0.7 constant_dynamic-slice_fusion
  (12 shorter events, 0.1 us)
Async XLA Ops:
  0.6 2.0 %copy-start = (s32[100,16,128]{2,1,0:T(8,128)S(1)}, s32[100,16,128]{2,1,0:T(8,128)}, u32[]{:S(2)}) copy-start(s32[100,16,128]{2,1,0:T(8,128)} %param.3) | copy-start | bytes 2457604
  4.5 33.0 %all-to-all-start = ((bf16[2,100,16,8,16]{1,4,2,0,3:T(8,128)(2,1)}), bf16[2,100,16,8,16]{1,4,2,0,3:T(8,128)(2,1)S(1)}, u32[]{:S(2)}, u32[]{:S(2)}) async-start(bf16[2,100,16,8,16]{1,4,2,0,3:T(8,128)(2,1)} %copy.75), calls=%async_computation | async-start | bytes 2097152 | tf_op jit(solution)/shard_map/all_to_all | solution.py:55
  57.2 7.3 %collective-permute-start = (f32[2,16,16]{1,2,0:T(8,128)S(1)}, f32[2,16,16]{1,2,0:T(8,128)S(1)}, u32[]{:S(2)}, u32[]{:S(2)}) collective-permute-start(f32[2,16,16]{1,2,0:T(8,128)S(1)} %get-tuple-element.27), channel_id=1, source_target_pairs={{0,14},{2,0},{4,2},{6,4},{8,6},{10,8},{12,10},{14,12},{1,15},{3,1}... | collective-permute-start | bytes 6152 | tf_op jit(solution)/shard_map/ppermute | solution.py:73
  59.6 5.0 %collective-permute-start.1 = (f32[2,16,16]{1,2,0:T(8,128)S(1)}, f32[2,16,16]{1,2,0:T(8,128)S(1)}, u32[]{:S(2)}, u32[]{:S(2)}) collective-permute-start(f32[2,16,16]{1,2,0:T(8,128)S(1)} %get-tuple-element.26), channel_id=1, source_target_pairs={{0,12},{2,14},{4,0},{6,2},{8,4},{10,6},{12,8},{14,10},{1,13},{3,15... | collective-permute-start | bytes 6152 | tf_op jit(solution)/shard_map/ppermute | solution.py:73
  59.6 7.7 %collective-permute-start.2 = (f32[2,16,16]{1,2,0:T(8,128)S(1)}, f32[2,16,16]{1,2,0:T(8,128)S(1)}, u32[]{:S(2)}, u32[]{:S(2)}) collective-permute-start(f32[2,16,16]{1,2,0:T(8,128)S(1)} %get-tuple-element.25), channel_id=1, source_target_pairs={{0,10},{2,12},{4,14},{6,0},{8,2},{10,4},{12,6},{14,8},{1,11},{3,13... | collective-permute-start | bytes 6152 | tf_op jit(solution)/shard_map/ppermute | solution.py:73
  59.8 7.6 %collective-permute-start.3 = (f32[2,16,16]{1,2,0:T(8,128)S(1)}, f32[2,16,16]{1,2,0:T(8,128)S(1)}, u32[]{:S(2)}, u32[]{:S(2)}) collective-permute-start(f32[2,16,16]{1,2,0:T(8,128)S(1)} %get-tuple-element.24), channel_id=1, source_target_pairs={{0,8},{2,10},{4,12},{6,14},{8,0},{10,2},{12,4},{14,6},{1,9},{3,11}... | collective-permute-start | bytes 6152 | tf_op jit(solution)/shard_map/ppermute | solution.py:73
  62.9 5.5 %collective-permute-start.4 = (f32[2,16,16]{1,2,0:T(8,128)S(1)}, f32[2,16,16]{1,2,0:T(8,128)S(1)}, u32[]{:S(2)}, u32[]{:S(2)}) collective-permute-start(f32[2,16,16]{1,2,0:T(8,128)S(1)} %get-tuple-element.23), channel_id=1, source_target_pairs={{0,6},{2,8},{4,10},{6,12},{8,14},{10,0},{12,2},{14,4},{1,7},{3,9},... | collective-permute-start | bytes 6152 | tf_op jit(solution)/shard_map/ppermute | solution.py:73
  64.6 5.5 %collective-permute-start.5 = (f32[2,16,16]{1,2,0:T(8,128)S(1)}, f32[2,16,16]{1,2,0:T(8,128)S(1)}, u32[]{:S(2)}, u32[]{:S(2)}) collective-permute-start(f32[2,16,16]{1,2,0:T(8,128)S(1)} %get-tuple-element.22), channel_id=1, source_target_pairs={{0,4},{2,6},{4,8},{6,10},{8,12},{10,14},{12,0},{14,2},{1,5},{3,7},... | collective-permute-start | bytes 6152 | tf_op jit(solution)/shard_map/ppermute | solution.py:73
  64.6 6.5 %collective-permute-start.6 = (f32[2,16,16]{1,2,0:T(8,128)S(1)}, f32[2,16,16]{1,2,0:T(8,128)S(1)}, u32[]{:S(2)}, u32[]{:S(2)}) collective-permute-start(f32[2,16,16]{1,2,0:T(8,128)S(1)} %get-tuple-element.21), channel_id=1, source_target_pairs={{0,2},{2,4},{4,6},{6,8},{8,10},{10,12},{12,14},{14,0},{1,3},{3,5},... | collective-permute-start | bytes 6152 | tf_op jit(solution)/shard_map/ppermute | solution.py:73
